TPU v7x, 32 devices: a whole 2x2x4 slice. The times are simulated.
32 devices in a mesh: dp: 2 (over x), tp: 4 (over z), ep: 4 (over y, core).
Axes of the slice: x: 2, y: 2, z: 4, core: 2. Of those that a mesh axis runs over, the one named last changes fastest.
Arguments:
- tokens: bfloat16 [16384, 1024], P(('dp', 'ep', 'tp')), parts along dimension 0
- expert_ids: int32 [16384, 8], P(('dp', 'ep', 'tp')), parts along dimension 0
- gates: float32 [16384, 8], P(('dp', 'ep', 'tp')), parts along dimension 0
- w_gate: bfloat16 [32, 1024, 512], P('ep', None, 'tp')
- w_up: bfloat16 [32, 1024, 512], P('ep', None, 'tp')
- w_down: bfloat16 [32, 512, 1024], P('ep', 'tp')
Outputs:
- output: bfloat16 [16384, 1024], P(('dp', 'ep', 'tp')), parts along dimension 0
There are 2 independent parts. A program takes and returns all parts, laid end to end along the dimension named above; an argument that names none is the same for every part.
All inputs are finite; a program needn't handle non-finite values.
Results may differ from a plain program's by a relative error of at most 0.001.
Values are sent between devices in bfloat16 or wider.
A program may use at most 1 GiB of HBM per device.

v0:
```python
import functools

import jax
import jax.numpy as jnp
from jax import lax
from jax.experimental import pallas as pl
from jax.experimental.pallas import tpu as pltpu
from jax.sharding import PartitionSpec as P

MESH = pl.DeviceIdType.MESH
F32 = jnp.float32
BF16 = jnp.bfloat16

PIECES = 4
COLS = 256


def layer_kernel(
    tok_h, ids_ref, gates_ref, wg_h, wu_h, wd_h, out_ref,
    tok, raw, gm, wg, wu, wd, hid, acc, got_a, got_b, got_c,
    loc_sem, tok_ss, tok_rs, own_ss, own_rs, z_ss, z_rs, x_ss, x_rs, cz_ss, cz_rs, cx_ss, cx_rs, out_ss, out_rs,
):
    n_own, hidden, ff = wg_h.shape
    half = n_own // 2
    rows = tok_h.shape[0]
    part = rows // 2
    n_cols = hidden // COLS
    chunk = rows // PIECES
    top_k = ids_ref.shape[0]
    x = lax.axis_index("dp")
    z = lax.axis_index("tp")
    ep = lax.axis_index("ep")
    core = lax.rem(ep, 2)
    to_x = {"dp": 1 - x}
    to_y = {"ep": lax.rem(ep + 2, 4)}
    to_c = {"ep": ep + 1 - 2 * core}
    to_z = {"tp": z + 1 - 2 * lax.rem(z, 2)}
    to_zz = {"tp": lax.rem(z + 2, 4)}
    row_d, row_c, row_b, row_a = 0, rows, 2 * rows, 3 * rows

    def rcopy(src, dst, ss, rs, dev):
        return pltpu.make_async_remote_copy(
            src_ref=src, dst_ref=dst, send_sem=ss, recv_sem=rs, device_id=dev, device_id_type=MESH
        )

    bufs = (wg, wu, wd)
    hbm = (wg_h, wu_h, wd_h)

    loc = [pltpu.make_async_copy(tok_h, tok.at[pl.ds(row_d, rows)], loc_sem.at[0])]
    loc += [pltpu.make_async_copy(hbm[a], bufs[a].at[0, 0], loc_sem.at[1 + a]) for a in range(3)]
    for cp in loc:
        cp.start()
    raw[0, pl.ds(0, top_k)] = ids_ref[...].astype(F32)
    raw[0, pl.ds(top_k, top_k)] = gates_ref[...]

    barrier = pltpu.get_barrier_semaphore()
    for dev in (to_x, to_y, to_c, to_z, to_zz):
        pl.semaphore_signal(barrier, inc=1, device_id=dev, device_id_type=MESH)
    with jax.named_scope("entry"):
        pl.semaphore_wait(barrier, 5)

    def side(base, p):
        return pl.ds(base + p * part, part)

    tok_y = [rcopy(tok_h.at[side(0, p)], tok.at[side(row_c, p)], tok_ss.at[8 * p], tok_rs.at[8 * p], to_y)
             for p in range(2)]
    gat_y = rcopy(raw.at[0], raw.at[1], tok_ss.at[1], tok_rs.at[1], to_y)
    gat_z = rcopy(raw.at[0], raw.at[2], tok_ss.at[2], tok_rs.at[2], to_zz)
    gat_f = rcopy(raw.at[2], raw.at[3], tok_ss.at[3], tok_rs.at[3], to_y)
    tok_z = [rcopy(tok_h.at[side(0, p)], tok.at[side(row_b, p)], tok_ss.at[4 + p], tok_rs.at[4 + p], to_zz)
             for p in range(2)]
    tok_f = [rcopy(tok.at[side(row_b, p)], tok.at[side(row_a, p)], tok_ss.at[6 + p], tok_rs.at[6 + p], to_y)
             for p in range(2)]

    def own_c(i, a):
        return rcopy(hbm[a].at[i], bufs[a].at[0, 1, i], own_ss.at[i, a], own_rs.at[i, a], to_c)

    n_in = 2 * half
    n_z = n_in + n_cols

    def at_slot(share, n, lo):
        if n < n_in:
            return bufs[n % 2].at[1, share, lo + n // 2]
        return wd.at[1, share, pl.ds(lo, half), :, pl.ds((n - n_in) * COLS, COLS)]

    def over_z(n):
        if n < n_in:
            src = hbm[n % 2].at[x * half + n // 2]
        else:
            src = wd_h.at[pl.ds(x * half, half), :, pl.ds((n - n_in) * COLS, COLS)]
        return rcopy(src, at_slot(0, n, 0), z_ss.at[n], z_rs.at[n], to_z)

    def over_x(n):
        return rcopy(at_slot(0, n, 0), at_slot(0, n, half), x_ss.at[n], x_rs.at[n], to_x)

    def over_cz(n):
        return rcopy(at_slot(0, n, 0), at_slot(1, n, 0), cz_ss.at[n], cz_rs.at[n], to_c)

    def over_cx(n):
        return rcopy(at_slot(0, n, half), at_slot(1, n, half), cx_ss.at[n], cx_rs.at[n], to_c)

    inner_layer = lax.rem(z * (3 - z), 3) // 2
    tok_z[0].start()
    tok_y[0].start()
    gat_z.start()
    gat_y.start()
    tok_y[1].start()

    @pl.when(inner_layer == 0)
    def _():
        tok_z[1].start()

    for a in range(3):
        own_c(0, a).start()
    for n in range(n_z):
        over_z(n).start()
    for i in range(1, n_own):
        for a in range(3):
            own_c(i, a).start()

    base = (ep * n_own, (ep + 1 - 2 * core) * n_own)

    def gates_of(b):
        lane = lax.broadcasted_iota(jnp.int32, (2 * n_own, rows), 0)
        second_core = lane >= n_own
        t = jnp.where(second_core, lane - n_own, lane) + x * half
        t = jnp.where(t >= n_own, t - n_own, t)
        name = (t + jnp.where(second_core, base[1], base[0])).astype(F32)
        mine_of = jnp.zeros(name.shape, F32)
        for j in range(top_k):
            mine_of += jnp.where(name == raw[b, j : j + 1], raw[b, top_k + j : top_k + j + 1], 0.0)
        full = jnp.concatenate([mine_of, jnp.zeros((128 - 2 * n_own, rows), F32)], axis=0)
        gm[pl.ds(b * rows, rows)] = full.T

    with jax.named_scope("loc"):
        for cp in loc:
            cp.wait()
    gates_of(0)

    def slot(t):
        return (t % 2) * half + t // 2

    def inner(r, m, s, i):
        at = pl.ds(pl.multiple_of(r, m), m)
        xb = tok[at]
        for c in range(2):
            w_in = jnp.concatenate([wg[s, c, i], wu[s, c, i]], axis=1)
            both = jnp.dot(xb, w_in, preferred_element_type=F32)
            hid[s, c, i, at] = (jax.nn.silu(both[:, :ff]) * both[:, ff:]).astype(BF16)

    def first(r, m):
        def go(i, carry):
            inner(r, m, 0, i)
            return carry

        lax.fori_loop(0, n_own, go, 0)

    def second(r, m, lo, hi):
        def go(t, carry):
            inner(r, m, 1, slot(t))
            return carry

        lax.fori_loop(lo, hi, go, 0)

    def second_blocks(t, lo, hi):
        def go(b, carry):
            inner(b * rows, rows, 1, slot(t))
            return carry

        lax.fori_loop(lo, hi, go, 0)

    def down(r, k):
        at = pl.ds(r, rows)
        sl = pl.ds(pl.multiple_of(k * COLS, COLS), COLS)
        for q in range(n_own):
            i = lax.rem(x * half + q, n_own)
            total = None if q == 0 else acc[k, at]
            for c in range(2):
                h = jnp.concatenate([hid[0, c, i, at], hid[1, c, q, at]], axis=1)
                w_out = jnp.concatenate([wd[0, c, i, :, sl], wd[1, c, q, :, sl]], axis=0)
                lane = c * n_own + q
                term = gm[at, lane : lane + 1] * jnp.dot(h, w_out, preferred_element_type=F32)
                total = term if total is None else total + term
            acc[k, at] = total

    def pass_z(n):
        with jax.named_scope(f"ev_z{n}"):
            over_z(n).wait_recv()
        over_x(n).start()
        over_cz(n).start()

    def pass_x(n):
        with jax.named_scope(f"ev_x{n}"):
            over_x(n).wait_recv()
        over_cx(n).start()

    def ready(t):
        with jax.named_scope(f"ev_q{t}"):
            for n in (t - t % 2, t - t % 2 + 1):
                (over_cx(n) if t % 2 else over_cz(n)).wait_recv()

    def rows_of(j):
        return pl.ds(j * chunk, chunk)

    def out_copy(which, r, got, dev):
        def make(k, j):
            return rcopy(acc.at[k, pl.ds(r + j * chunk, chunk)], got.at[k, rows_of(j)],
                         out_ss.at[which, k, j], out_rs.at[which, k, j], dev)

        return make

    send_a = out_copy(0, row_a, got_a, to_y)
    send_b = out_copy(1, row_b, got_b, to_zz)
    send_c = out_copy(2, row_c, got_c, to_y)

    def add_a(k, j):
        with jax.named_scope(f"late_a{k}{j}"):
            send_a(k, j).wait_recv()
        at = pl.ds(row_b + j * chunk, chunk)
        acc[k, at] = acc[k, at] + got_a[k, rows_of(j)]
        send_b(k, j).start()

    def give(k, j):
        with jax.named_scope(f"late_c{k}{j}"):
            send_c(k, j).wait_recv()
        with jax.named_scope(f"late_b{k}{j}"):
            send_b(k, j).wait_recv()
        total = acc[k, rows_of(j)] + got_c[k, rows_of(j)] + got_b[k, rows_of(j)]
        out_ref[rows_of(j), pl.ds(k * COLS, COLS)] = total.astype(out_ref.dtype)

    def mine(i, carry):
        with jax.named_scope("ev_own"):
            for a in range(3):
                own_c(i, a).wait_recv()
        inner(row_d, rows, 0, i)
        return carry

    lax.fori_loop(0, n_own, mine, 0)

    def near_tokens(p):
        with jax.named_scope(f"ev_tok_c{p}"):
            tok_y[p].wait_recv()
            if p == 0:
                gat_y.wait_recv()
        if p == 0:
            gates_of(1)
        first(row_c + p * part, part)

    def b_tokens(p):
        with jax.named_scope(f"ev_tok_b{p}"):
            tok_z[p].wait_recv()
            if p == 0:
                gat_z.wait_recv()
        tok_f[p].start()
        if p == 0:
            gat_f.start()
            gates_of(2)

    def a_tokens(p):
        with jax.named_scope(f"ev_tok_a{p}"):
            tok_f[p].wait_recv()
            if p == 0:
                gat_f.wait_recv()
        if p == 0:
            gates_of(3)
        first(row_a + p * part, part)

    def middle():
        tok_z[1].start()
        near_tokens(0)
        near_tokens(1)
        b_tokens(0)
        pass_z(0)
        first(row_b, part)
        pass_z(1)
        ready(0)
        second_blocks(0, 0, 2)
        second(row_b, part, 0, 1)
        pass_z(2)
        a_tokens(0)
        pass_x(0)
        pass_x(1)
        b_tokens(1)
        pass_z(3)
        first(row_b + part, part)
        ready(1)
        second_blocks(1, 0, 2)
        second(row_b, part, 1, 2)
        second(row_b + part, part, 0, 2)
        pass_z(4)
        ready(2)
        second_blocks(2, 0, 3)
        pass_x(2)
        pass_x(3)
        second(row_a, part, 0, 3)
        pass_z(5)
        a_tokens(1)
        second(row_a + part, part, 0, 3)
        ready(3)
        second_blocks(3, 0, 2)
        pass_z(6)
        second_blocks(3, 2, 4)
        pass_x(4)
        pass_x(5)
        ready(4)
        second_blocks(4, 1, 4)
        pass_z(7)
        ready(5)
        second_blocks(5, 1, 4)
        ready(6)
        second_blocks(6, 2, 4)
        pass_z(8)
        pass_x(6)
        pass_x(7)
        ready(7)
        second_blocks(7, 2, 4)
        pass_z(9)

    def end():
        pass_z(0)
        near_tokens(0)
        pass_z(1)
        near_tokens(1)
        pass_z(2)
        pass_x(0)
        pass_x(1)
        ready(0)
        second_blocks(0, 0, 2)
        ready(1)
        second_blocks(1, 0, 2)
        b_tokens(0)
        first(row_b, part)
        second(row_b, part, 0, 2)
        b_tokens(1)
        pass_z(3)
        first(row_b + part, part)
        second(row_b + part, part, 0, 2)
        pass_z(4)
        a_tokens(0)
        second(row_a, part, 0, 2)
        ready(2)
        second_blocks(2, 1, 3)
        second(row_a, part, 2, 3)
        pass_x(2)
        pass_x(3)
        pass_z(5)
        ready(3)
        second_blocks(3, 1, 3)
        second(row_a, part, 3, 4)
        a_tokens(1)
        pass_z(6)
        second(row_a + part, part, 0, 4)
        pass_x(4)
        pass_x(5)
        ready(4)
        second_blocks(4, 1, 4)
        pass_z(7)
        ready(5)
        second_blocks(5, 1, 4)
        ready(6)
        second_blocks(6, 2, 4)
        pass_z(8)
        pass_x(6)
        pass_x(7)
        ready(7)
        second_blocks(7, 2, 4)
        pass_z(9)

    pl.when(inner_layer == 1)(middle)
    pl.when(inner_layer == 0)(end)

    def column(k, carry):
        for m in range(n_cols):
            @pl.when(k == m)
            def _(m=m):
                n = n_in + m
                if m == 0:
                    pass_x(n)
                with jax.named_scope(f"ev_w{m}"):
                    over_cz(n).wait_recv()
                    over_cx(n).wait_recv()

        down(row_a, k)
        with jax.named_scope("out_a"):
            for j in range(PIECES):
                send_a(k, j).start()

        @pl.when(k == 1)
        def _():
            add_a(0, 1)

        down(row_b, k)

        @pl.when(k == 0)
        def _():
            put_off = 2 + 2 * inner_layer
            second(row_d, rows, put_off, put_off + 3)
            add_a(0, 0)
            pass_z(n_in + 2)
            second(row_d, rows, put_off + 3, n_own)
            second(row_c, rows, n_own - 2, n_own)

        @pl.when(k == 1)
        def _():
            add_a(0, 2)

        @pl.when(k == 2)
        def _():
            add_a(0, 3)

        down(row_c, k)
        for now, blocks in ((0, (0,)), (2, (1,)), (3, (2, 3))):
            @pl.when(k == now)
            def _(blocks=blocks):
                for m in blocks:
                    for j in range(PIECES):
                        send_c(m, j).start()

        for m in range(1, n_cols):
            @pl.when(k == m - 1)
            def _(m=m):
                if m == 1:
                    pass_z(n_in + 3)
                pass_x(n_in + m)

        down(row_d, k)
        return carry

    lax.fori_loop(0, n_cols, column, 0)
    for add_k, give_k in ((1, 0), (2, None), (3, 1), (None, 2), (None, 3)):
        for j in range(PIECES):
            if give_k is not None:
                give(give_k, j)
            if add_k is not None:
                add_a(add_k, j)

    for cp in [gat_y, gat_z, gat_f] + tok_y + tok_z + tok_f:
        cp.wait_send()
    for a in range(3):
        for i in range(n_own):
            own_c(i, a).wait_send()
    for n in range(n_z):
        for cp in (over_z(n), over_x(n), over_cz(n), over_cx(n)):
            cp.wait_send()
    for k in range(n_cols):
        for j in range(PIECES):
            for cp in (send_a(k, j), send_b(k, j), send_c(k, j)):
                cp.wait_send()


def solution(mesh):
    row_spec = P(("dp", "ep", "tp"), None)

    def local_layer(tokens, expert_ids, gates, w_gate, w_up, w_down):
        n_own = w_gate.shape[0]
        rows, hidden = tokens.shape
        ff = w_gate.shape[2]
        n_cols = hidden // COLS
        n_z = n_own + n_cols
        any_spec = pl.BlockSpec(memory_space=pl.ANY)
        vmem_spec = pl.BlockSpec(memory_space=pltpu.VMEM)
        dma = pltpu.SemaphoreType.DMA
        return pl.pallas_call(
            layer_kernel,
            out_shape=jax.ShapeDtypeStruct((rows, hidden), jnp.bfloat16),
            in_specs=[any_spec, vmem_spec, vmem_spec, any_spec, any_spec, any_spec],
            out_specs=vmem_spec,
            scratch_shapes=[
                pltpu.VMEM((4 * rows, hidden), BF16),
                pltpu.VMEM((4, 2 * expert_ids.shape[1], rows), F32),
                pltpu.VMEM((4 * rows, 128), F32),
                pltpu.VMEM((2, 2, n_own, hidden, ff), BF16),
                pltpu.VMEM((2, 2, n_own, hidden, ff), BF16),
                pltpu.VMEM((2, 2, n_own, ff, hidden), BF16),
                pltpu.VMEM((2, 2, n_own, 4 * rows, ff), BF16),
                pltpu.VMEM((n_cols, 4 * rows, COLS), F32),
                pltpu.VMEM((n_cols, rows, COLS), F32),
                pltpu.VMEM((n_cols, rows, COLS), F32),
                pltpu.VMEM((n_cols, rows, COLS), F32),
                dma((4,)), dma((9,)), dma((9,)),
                dma((n_own, 3)), dma((n_own, 3)),
                dma((n_z,)), dma((n_z,)), dma((n_z,)), dma((n_z,)),
                dma((n_z,)), dma((n_z,)), dma((n_z,)), dma((n_z,)),
                dma((3, n_cols, PIECES)), dma((3, n_cols, PIECES)),
            ],
            compiler_params=pltpu.CompilerParams(
                collective_id=0, has_side_effects=True, vmem_limit_bytes=67_043_328
            ),
        )(tokens, expert_ids.T, gates.T, w_gate, w_up, w_down)

    return jax.shard_map(local_layer, mesh=mesh, in_specs=(row_spec, row_spec, row_spec, P("ep", None, "tp"), P("ep", None, "tp"), P("ep", "tp", None)), out_specs=row_spec, check_vma=False)
```

profile of v0, /device:TPU:0, one launch (start us, length us, event | category | flops | bytes accessed | tf_op | source)
XLA Modules:
  0.0 195.6 jit_solution(2549236710787865196)
XLA Ops:
  0.0 193.3 %shard_map.64 = bf16[512,1024]{1,0:T(8,128)(2,1)} custom-call(bf16[512,1024]{1,0:T(8,128)(2,1)} %tok_h.1, s32[8,512]{1,0:T(8,128)} %bitcast.2, f32[8,512]{1,0:T(8,128)} %bitcast.3, bf16[8,1024,128]{2,1,0:T(8,128)(2,1)} %wg_h.1, bf16[8,1024,128]{2,1,0:T(8,128)(2,1)} %wu_h.1, bf16[8,128,1024]{2,1,0:T(8,128)(2,1)} %wd_h.1), custom_call_target="tpu_custom_call" | custom-call | tf_op jit(solution)/shard_map/pallas_call | solution.py:463
  193.3 2.3 %copy.8 = bf16[512,1024]{1,0:T(8,128)(2,1)} copy(bf16[512,1024]{1,0:T(8,128)(2,1)} %shard_map.64) | data formatting | bytes 2097152
where the time goes:
time: 196 us
  Pallas kernels  193 us (98%)
  local copies, waits for them, and re-layouts  2.26 us (1%)
    pallas_call x1, Pallas kernels, local_layer(): pl.pallas_call(layer_kernel, out_shape=jax.ShapeDtypeStruct((rows, hidden...  193 us

commit v1 on v0

--- a/solution.py
+++ b/solution.py
@@ -408,8 +408,13 @@
         def _():
             add_a(0, 3)
 
+        @pl.when(k == 3)
+        def _():
+            add_a(1, 0)
+            add_a(1, 1)
+
         down(row_c, k)
-        for now, blocks in ((0, (0,)), (2, (1,)), (3, (2, 3))):
+        for now, blocks in ((1, (0,)), (2, (1,)), (3, (2, 3))):
             @pl.when(k == now)
             def _(blocks=blocks):
                 for m in blocks:
@@ -427,7 +432,9 @@
         return carry
 
     lax.fori_loop(0, n_cols, column, 0)
-    for add_k, give_k in ((1, 0), (2, None), (3, 1), (None, 2), (None, 3)):
+    add_a(1, 2)
+    add_a(1, 3)
+    for add_k, give_k in ((2, 0), (3, 1), (None, 2), (None, 3)):
         for j in range(PIECES):
             if give_k is not None:
                 give(give_k, j)

time: 196 us -> 196 us (level)
  no operation moved by 1% of the time
where the time goes in v1:
time: 196 us; the launch traced here: 195 us
  Pallas kernels  193 us (98%)
  local copies, waits for them, and re-layouts  2.26 us (1%)
    pallas_call x1, Pallas kernels, local_layer(): pl.pallas_call(layer_kernel, out_shape=jax.ShapeDtypeStruct((rows, hidden...  193 us

profile of v1, /device:TPU:0, one launch (start us, length us, event | category | flops | bytes accessed | tf_op | source)
XLA Modules:
  0.0 195.3 jit_solution(1982966263588750307)
XLA Ops:
  0.0 193.0 %shard_map.64 = bf16[512,1024]{1,0:T(8,128)(2,1)} custom-call(bf16[512,1024]{1,0:T(8,128)(2,1)} %tok_h.1, s32[8,512]{1,0:T(8,128)} %bitcast.2, f32[8,512]{1,0:T(8,128)} %bitcast.3, bf16[8,1024,128]{2,1,0:T(8,128)(2,1)} %wg_h.1, bf16[8,1024,128]{2,1,0:T(8,128)(2,1)} %wu_h.1, bf16[8,128,1024]{2,1,0:T(8,128)(2,1)} %wd_h.1), custom_call_target="tpu_custom_call" | custom-call | tf_op jit(solution)/shard_map/pallas_call | solution.py:470
  193.0 2.3 %copy.8 = bf16[512,1024]{1,0:T(8,128)(2,1)} copy(bf16[512,1024]{1,0:T(8,128)(2,1)} %shard_map.64) | data formatting | bytes 2097152
